TPU v7x, 8 devices: a whole 2x2x1 slice. The times are simulated.
8 devices in a mesh: data: 1 (over z), row: 2 (over y), col: 4 (over x, core).
Axes of the slice: x: 2, y: 2, z: 1, core: 2. Of those that a mesh axis runs over, the one named last changes fastest.
Arguments:
- tokens: bfloat16 [1024, 2048], P(('data', 'row', 'col'))
- expert_ids: int32 [1024, 8], P(('data', 'row', 'col'))
- gate_weights: float32 [1024, 8], P(('data', 'row', 'col'))
- w_in: bfloat16 [256, 2048, 512], P(('row', 'col'))
- w_out: bfloat16 [256, 512, 2048], P(('row', 'col'))
Outputs:
- output: bfloat16 [1024, 2048], P(('data', 'row', 'col'))
All inputs are finite; a program needn't handle non-finite values.
Results may differ from a plain program's by a relative error of at most 0.00450213.
Values are sent between devices in bfloat16 or wider.
A program may use at most 1 GiB of HBM per device.

v0:
```python
import jax
import jax.numpy as jnp
from jax import lax
from jax.sharding import PartitionSpec as P

GRID_AXES = ('row', 'col')


def local_ranks(flat_ids, num_experts):
    pair_count = flat_ids.shape[0]
    sort_order = jnp.argsort(flat_ids, stable=True)
    counts = jnp.zeros((num_experts,), jnp.int32).at[flat_ids].add(1)
    starts = jnp.cumsum(counts) - counts
    sorted_rank = jnp.arange(pair_count, dtype=jnp.int32) - starts[flat_ids[sort_order]]
    pair_rank = jnp.zeros((pair_count,), jnp.int32).at[sort_order].set(sorted_rank)
    return counts, pair_rank


def solution(mesh):
    rows_n = mesh.shape['row']
    cols_n = mesh.shape['col']
    group_size = rows_n * cols_n

    def device_fn(tokens, expert_ids, gate_weights, w_in, w_out):
        tok_dev, model_width = tokens.shape
        top_k = expert_ids.shape[1]
        local_experts = w_in.shape[0]
        num_experts = local_experts * group_size
        capacity = tok_dev * group_size * top_k // num_experts
        per_source = 2 * tok_dev * top_k // num_experts
        flat_ids = expert_ids.reshape(-1)
        pair_count = flat_ids.shape[0]
        counts, pair_rank = local_ranks(flat_ids, num_experts)

        col_counts = lax.all_gather(counts, 'col')
        col_before = jnp.arange(cols_n)[:, None] < lax.axis_index('col')
        before_col = jnp.sum(jnp.where(col_before, col_counts, 0), axis=0)
        row_totals = lax.all_gather(jnp.sum(col_counts, axis=0), 'row')
        row_before = jnp.arange(rows_n)[:, None] < lax.axis_index('row')
        before_row = jnp.sum(jnp.where(row_before, row_totals, 0), axis=0)
        offsets = before_row + before_col

        global_rank = offsets[flat_ids] + pair_rank
        send_pos = flat_ids * per_source + pair_rank
        send_token = jnp.where(global_rank < capacity, jnp.arange(pair_count, dtype=jnp.int32) // top_k, tok_dev)
        send_index = jnp.full((num_experts * per_source,), tok_dev, jnp.int32).at[send_pos].set(send_token)
        send_rows = jnp.take(tokens, send_index, axis=0, mode='fill', fill_value=0)
        send_rows = send_rows.reshape(group_size, local_experts, per_source, model_width)
        meta_send = jnp.stack([offsets, counts], axis=-1).reshape(group_size, local_experts, 2)

        meta_recv = lax.all_to_all(meta_send, GRID_AXES, 0, 0, tiled=True)
        recv_rows = lax.all_to_all(send_rows, GRID_AXES, 0, 0, tiled=True)

        source_off = meta_recv[:, :, 0]
        source_cnt = meta_recv[:, :, 1]
        source_end = source_off + source_cnt
        slot_pos = jnp.arange(capacity)
        slot_source = jnp.sum(source_end.T[:, None, :] <= slot_pos[None, :, None], axis=-1)
        source_clip = jnp.minimum(slot_source, group_size - 1)
        slot_start = jnp.take_along_axis(source_off.T, source_clip, axis=1)
        expert_pos = jnp.arange(local_experts)[:, None]
        recv_index = (source_clip * local_experts + expert_pos) * per_source + slot_pos[None, :] - slot_start
        recv_index = jnp.where(slot_source < group_size, recv_index, group_size * local_experts * per_source)
        buffer = jnp.take(recv_rows.reshape(-1, model_width), recv_index.reshape(-1), axis=0, mode='fill', fill_value=0)
        buffer = buffer.reshape(local_experts, capacity, model_width)

        hidden = jax.nn.gelu(jnp.einsum('ecd,edf->ecf', buffer, w_in, preferred_element_type=jnp.float32)).astype(jnp.bfloat16)
        expert_out = jnp.einsum('ecf,efd->ecd', hidden, w_out, preferred_element_type=jnp.float32).astype(jnp.bfloat16)

        back_pos = jnp.arange(per_source)
        back_slot = source_off[:, :, None] + back_pos
        back_valid = (back_pos < source_cnt[:, :, None]) & (back_slot < capacity)
        back_index = jnp.where(back_valid, jnp.arange(local_experts)[None, :, None] * capacity + back_slot, local_experts * capacity)
        back_rows = jnp.take(expert_out.reshape(-1, model_width), back_index.reshape(-1), axis=0, mode='fill', fill_value=0)
        back_rows = back_rows.reshape(group_size, local_experts, per_source, model_width)
        returned = lax.all_to_all(back_rows, GRID_AXES, 0, 0, tiled=True)

        pair_rows = jnp.take(returned.reshape(-1, model_width), send_pos, axis=0, mode='fill', fill_value=0).reshape(tok_dev, top_k, model_width)
        mixed_sum = jnp.einsum('tk,tkd->td', gate_weights, pair_rows, preferred_element_type=jnp.float32)
        return (tokens.astype(jnp.float32) + mixed_sum).astype(jnp.bfloat16)

    token_spec = P(('data', 'row', 'col'), None)
    expert_spec = P(GRID_AXES, None, None)
    return jax.shard_map(device_fn, mesh=mesh, in_specs=(token_spec, token_spec, token_spec, expert_spec, expert_spec), out_specs=token_spec, check_vma=False)
```

profile of v0, /device:TPU:0, one launch (start us, length us, event | category | flops | bytes accessed | tf_op | source)
XLA Modules:
  0.0 380.9 jit_solution(17594303727474151852)
XLA Ops:
  0.0 0.8 copy.15
  0.8 0.1 reshape.262
  0.9 7.6 %scatter_custom_fusion = s32[256]{0:T(256)S(1)} fusion(s32[1024]{0:T(1024)S(1)} %bitcast.72, s32[1024]{0:T(1024)S(1)} %broadcast.213, s32[]{:T(128)} %constant.48.clone.1), kind=kCustom, calls=%fused_computation.92 | custom fusion | flops 1024 | bytes 1028 | tf_op jit(solution)/shard_map/scatter-add | solution.py:12
  8.5 0.1 stack.7
  8.6 9.8 %all-gather.2 = s32[4,1,256]{2,1,0:T(1,128)S(1)} all-gather(s32[1,1,256]{2,1,0:T(1,128)S(1)} %bitcast.70), channel_id=2, replica_groups=mesh['data'=1,'row'=2,'col'=4] {'col'}, dimensions={0}, use_global_device_ids=true | all-gather | bytes 5120 | tf_op jit(solution)/shard_map/all_gather | solution.py:35
  18.4 4.2 %all-gather.3 = s32[2,1,256]{2,1,0:T(1,128)S(1)} all-gather(s32[1,1,256]{2,1,0:T(1,128)S(1)} %bitcast.77), channel_id=3, replica_groups=mesh['data'=1,'row'=2,'col'=4] {'row'}, dimensions={0}, use_global_device_ids=true | all-gather | bytes 3072 | tf_op jit(solution)/shard_map/all_gather | solution.py:38
  22.7 0.1 fusion.28
  22.8 0.1 fusion.32
  22.9 0.1 add.186
  23.0 0.6 pad_add_fusion
  23.6 2.1 all-to-all-start
  25.6 0.1 reshape.263
  25.8 0.3 reduce-window.9
  26.1 0.1 slice.15
  26.2 0.1 slice_reduce_fusion
  26.3 0.1 bitcast_subtract_fusion
  26.4 4.4 %sort.17 = (s32[1024]{0:T(1024)}, s32[1024]{0:T(1024)S(1)}) sort(s32[1024]{0:T(1024)S(1)} %reshape.263, s32[1024]{0:T(1024)S(1)} %iota.43), dimensions={0}, to_apply=%region_4.5 | sort | flops 10240 | bytes 16384 | tf_op jit(solution)/shard_map/jit(argsort)/sort | solution.py:11
  30.7 4.5 %gather_fusion = s32[1024]{0:T(1024)S(1)} fusion(s32[1024]{0:T(1024)S(1)} %reshape.263, s32[1024]{0:T(1024)S(1)} %get-tuple-element.14), kind=kCustom, calls=%fused_computation.2 | custom fusion | bytes 12288 | tf_op jit(solution)/shard_map/gather | solution.py:14
  35.3 0.0 copy-start
  35.3 6.8 %gather_fusion.1 = s32[1024]{0:T(1024)S(1)} fusion(s32[256]{0:T(256)S(1)} %bitcast_subtract_fusion, s32[1024]{0:T(1024)S(1)} %broadcast_clamp_fusion.4), kind=kCustom, calls=%fused_computation.3 | custom fusion | bytes 12288 | tf_op jit(solution)/shard_map/gather | solution.py:14
  42.2 6.8 %gather_fusion.2 = s32[1024]{0:T(1024)S(1)} fusion(s32[256]{0:T(256)S(1)} %add.185, s32[1024]{0:T(1024)S(1)} %broadcast_clamp_fusion.3), kind=kCustom, calls=%fused_computation.4 | custom fusion | bytes 12288 | tf_op jit(solution)/shard_map/gather | solution.py:43
  49.0 4.3 %scatter_custom_fusion.1 = s32[1024]{0:T(1024)S(1)} fusion(s32[1024]{0:T(1024)S(1)} %get-tuple-element.15, s32[1024]{0:T(1024)S(1)} %iota_subtract_fusion, s32[]{:T(128)} %constant.48.clone.1), kind=kCustom, calls=%fused_computation.86 | custom fusion | bytes 4100 | tf_op jit(solution)/shard_map/scatter | solution.py:15
  53.4 4.3 %scatter_custom_fusion.2 = s32[2048]{0:T(1024)S(1)} fusion(s32[1024]{0:T(1024)S(1)} %get-tuple-element.9, s32[1024]{0:T(1024)S(1)} %fusion.25, s32[]{:T(128)} %constant.61.clone.1), kind=kCustom, calls=%fused_computation.74 | custom fusion | bytes 8196 | tf_op jit(solution)/shard_map/scatter | solution.py:46
  57.7 0.1 broadcast_in_dim.111
  57.8 0.0 copy-done
  57.8 11.0 %gather_fusion.3 = bf16[2048,2048]{1,0:T(8,128)(2,1)} fusion(bf16[128,2048]{1,0:T(8,128)(2,1)S(1)} %copy-done, s32[2048]{0:T(1024)S(1)} %fusion.24), kind=kCustom, calls=%fused_computation.5 | custom fusion | bytes 16785408 | tf_op jit(solution)/shard_map/jit(_take)/gather | solution.py:47
  68.8 7.3 %broadcast_select_fusion = bf16[8,32,8,2048]{3,2,1,0:T(8,128)(2,1)} fusion(bf16[8,32,8,2048]{3,2,1,0:T(8,128)(2,1)} %bitcast.64, pred[8,32,8]{2,1,0:T(8,128)(4,1)S(1)} %broadcast_in_dim.111), kind=kLoop, calls=%fused_computation.11 | loop fusion | flops 4194304 | bytes 16779264 | tf_op jit(solution)/shard_map/jit(_take)/select_n | solution.py:47
  76.1 0.0 all-to-all-done
  76.1 3.9 %all-to-all-start.1 = ((bf16[8,32,8,2048]{3,2,1,0:T(8,128)(2,1)}), bf16[8,32,8,2048]{3,2,1,0:T(8,128)(2,1)}, u32[]{:S(2)}, u32[]{:S(2)}) async-start(bf16[8,32,8,2048]{3,2,1,0:T(8,128)(2,1)} %broadcast_select_fusion), calls=%async_computation.1 | async-start | bytes 16777216 | tf_op jit(solution)/shard_map/all_to_all | solution.py:52
  80.0 0.1 add.202
  80.1 0.1 add.205
  80.2 0.1 copy.19
  80.3 0.1 convert_reduce_fusion
  80.4 0.1 reshape.327
  80.5 0.1 min.22
  80.6 0.1 lt.188
  80.7 0.1 add_select_fusion
  80.8 0.1 select_n.142
  80.9 4.7 %gather_fusion.5 = s32[1024]{0:T(1024)S(1)} fusion(s32[32,8]{0,1:T(8,128)S(1)} %bitcast.60, s32[1024]{0:T(1024)S(1)} %reshape.327), kind=kCustom, calls=%fused_computation.7 | custom fusion | bytes 16384 | tf_op jit(solution)/shard_map/jit(take_along_axis)/gather | solution.py:60
  85.7 0.1 compare_and_fusion
  85.9 88.0 %all-to-all-done.1 = bf16[8,32,8,2048]{3,2,1,0:T(8,128)(2,1)} async-done(((bf16[8,32,8,2048]{3,2,1,0:T(8,128)(2,1)}), bf16[8,32,8,2048]{3,2,1,0:T(8,128)(2,1)}, u32[]{:S(2)}, u32[]{:S(2)}) %all-to-all-start.1) | async-done | bytes 8388640 | tf_op jit(solution)/shard_map/all_to_all | solution.py:52
  173.9 13.3 %gather_fusion.6 = bf16[1024,2048]{1,0:T(8,128)(2,1)} fusion(bf16[2048,2048]{1,0:T(8,128)(2,1)} %bitcast.13, s32[1024]{0:T(1024)S(1)} %broadcast_clamp_fusion.2), kind=kCustom, calls=%fused_computation.clone | custom fusion | bytes 8392704 | tf_op jit(solution)/shard_map/jit(_take)/gather | solution.py:64
  187.2 2.5 broadcast_select_fusion.2
  189.7 23.4 %fusion.58 = bf16[32,32,512]{2,1,0:T(8,128)(2,1)S(1)} fusion(bf16[32,32,2048]{2,1,0:T(8,128)(2,1)S(1)} %bitcast.65, bf16[32,2048,512]{2,1,0:T(8,128)(2,1)} %param.10), kind=kOutput, calls=%fused_computation.27.clone.clone.1 | convolution fusion | flops 2152202240 | bytes 72351744 | tf_op jit(solution)/shard_map/ecd,edf->ecf/dot_general | solution.py:67
  213.1 25.7 %convolution_convert_fusion = bf16[32,32,2048]{2,1,0:T(8,128)(2,1)} fusion(bf16[32,512,2048]{2,1,0:T(8,128)(2,1)} %param.11, bf16[32,32,512]{2,1,0:T(8,128)(2,1)S(1)} %fusion.58), kind=kOutput, calls=%fused_computation.18 | convolution fusion | flops 2149580800 | bytes 72351744 | tf_op jit(solution)/shard_map/ecf,efd->ecd/dot_general | solution.py:68
  238.8 19.1 %gather_fusion.4 = bf16[2048,2048]{1,0:T(8,128)(2,1)} fusion(bf16[1024,2048]{1,0:T(8,128)(2,1)} %bitcast.62, s32[2048]{0:T(1024)S(1)} %broadcast_clamp_fusion), kind=kCustom, calls=%fused_computation.6 | custom fusion | bytes 16785408 | tf_op jit(solution)/shard_map/jit(_take)/gather | solution.py:74
  257.8 7.3 %broadcast_select_fusion.1 = bf16[8,32,8,2048]{3,2,1,0:T(8,128)(2,1)} fusion(bf16[8,32,8,2048]{3,2,1,0:T(8,128)(2,1)} %bitcast.63, pred[8,32,8]{2,1,0:T(8,128)(4,1)S(1)} %compare_and_fusion), kind=kLoop, calls=%fused_computation.12 | loop fusion | flops 4194304 | bytes 16779264 | tf_op jit(solution)/shard_map/jit(_take)/select_n | solution.py:74
  265.1 0.0 copy-start.1
  265.1 4.0 %all-to-all-start.2 = ((bf16[8,32,8,2048]{3,2,1,0:T(8,128)(2,1)}), bf16[8,32,8,2048]{3,2,1,0:T(8,128)(2,1)}, u32[]{:S(2)}, u32[]{:S(2)}) async-start(bf16[8,32,8,2048]{3,2,1,0:T(8,128)(2,1)} %broadcast_select_fusion.1), calls=%async_computation.2 | async-start | bytes 16777216 | tf_op jit(solution)/shard_map/all_to_all | solution.py:76
  269.2 0.0 copy-done.1
  269.2 0.1 copy.20
  269.4 93.6 %all-to-all-done.2 = bf16[8,32,8,2048]{3,2,1,0:T(8,128)(2,1)} async-done(((bf16[8,32,8,2048]{3,2,1,0:T(8,128)(2,1)}), bf16[8,32,8,2048]{3,2,1,0:T(8,128)(2,1)}, u32[]{:S(2)}, u32[]{:S(2)}) %all-to-all-start.2) | async-done | bytes 8388640 | tf_op jit(solution)/shard_map/all_to_all | solution.py:76
  362.9 13.3 %gather_fusion.7 = bf16[1024,2048]{1,0:T(8,128)(2,1)} fusion(bf16[2048,2048]{1,0:T(8,128)(2,1)} %bitcast.18, s32[1024]{0:T(1024)S(1)} %broadcast_clamp_fusion.1), kind=kCustom, calls=%fused_computation.1.clone | custom fusion | bytes 8392704 | tf_op jit(solution)/shard_map/jit(_take)/gather | solution.py:78
  376.2 3.5 fusion
  379.7 1.2 fusion.14
  (30 shorter events, 0.2 us)
Async XLA Ops:
  23.6 52.5 %all-to-all-start = ((s32[8,32,2]{1,2,0:T(2,128)}), s32[8,32,2]{1,2,0:T(2,128)S(1)}, u32[]{:S(2)}, u32[]{:S(2)}) async-start(s32[8,32,2]{1,2,0:T(2,128)} %pad_add_fusion), calls=%async_computation | async-start | bytes 16384 | tf_op jit(solution)/shard_map/all_to_all | solution.py:51
  35.3 22.5 %copy-start = (bf16[128,2048]{1,0:T(8,128)(2,1)S(1)}, bf16[128,2048]{1,0:T(8,128)(2,1)}, u32[]{:S(2)}) copy-start(bf16[128,2048]{1,0:T(8,128)(2,1)} %param.7) | copy-start | bytes 1572868
  76.1 97.8 %all-to-all-start.1 = ((bf16[8,32,8,2048]{3,2,1,0:T(8,128)(2,1)}), bf16[8,32,8,2048]{3,2,1,0:T(8,128)(2,1)}, u32[]{:S(2)}, u32[]{:S(2)}) async-start(bf16[8,32,8,2048]{3,2,1,0:T(8,128)(2,1)} %broadcast_select_fusion), calls=%async_computation.1 | async-start | bytes 16777216 | tf_op jit(solution)/shard_map/all_to_all | solution.py:52
  265.1 4.1 %copy-start.1 = (f32[128,8]{0,1:T(8,128)S(1)}, f32[128,8]{0,1:T(8,128)}, u32[]{:S(2)}) copy-start(f32[128,8]{0,1:T(8,128)} %param.9) | copy-start | bytes 12292
  265.1 97.8 %all-to-all-start.2 = ((bf16[8,32,8,2048]{3,2,1,0:T(8,128)(2,1)}), bf16[8,32,8,2048]{3,2,1,0:T(8,128)(2,1)}, u32[]{:S(2)}, u32[]{:S(2)}) async-start(bf16[8,32,8,2048]{3,2,1,0:T(8,128)(2,1)} %broadcast_select_fusion.1), calls=%async_computation.2 | async-start | bytes 16777216 | tf_op jit(solution)/shard_map/all_to_all | solution.py:76
where the time goes:
time: 381 us
  waiting for transfers between devices  182 us (48%)
  local copies, waits for them, and re-layouts  90.4 us (24%)
  matrix products  52.6 us (14%)
  other arithmetic  32 us (8%)
  blocking collectives  14 us (4%)
  starting transfers between devices  9.99 us (3%)
    all_to_all x1, waiting for transfers between devices, device_fn(): returned = lax.all_to_all(back_rows, GRID_AXES, 0, 0, tiled=True)  93.6 us
    all_to_all x1, waiting for transfers between devices, device_fn(): recv_rows = lax.all_to_all(send_rows, GRID_AXES, 0, 0, tiled=True)  88 us
    dot_general x1, matrix products, device_fn(): jnp.einsum('ecf,efd->ecd', hidden, w_out, preferred_element_type=jnp.floa...  25.7 us
    dot_general x1, matrix products, device_fn(): jnp.einsum('ecd,edf->ecf', buffer, w_in, preferred_element_type=jnp.float32)  23.4 us
    gather x1, local copies, waits for them, and re-layouts, device_fn(): jnp.take(expert_out.reshape(-1, model_width), back_index.reshape(-1), axi...  19.1 us
    gather x1, local copies, waits for them, and re-layouts, device_fn(): jnp.take(recv_rows.reshape(-1, model_width), recv_index.reshape(-1), axis...  13.3 us
    gather x1, local copies, waits for them, and re-layouts, device_fn(): jnp.take(returned.reshape(-1, model_width), send_pos, axis=0, mode='fill'...  13.3 us
    gather x1, local copies, waits for them, and re-layouts, device_fn(): send_rows = jnp.take(tokens, send_index, axis=0, mode='fill', fill_value=0)  11 us
  transfers between devices with their start and end apart: 3, of which 2 were waited for; matrix products, arithmetic and copies ran while one was open for 15% of the time, Pallas kernels for 0%

commit v1 on v0

v1 whole, which is shorter than its diff:
```python
import jax
import jax.numpy as jnp
from jax import lax
from jax.experimental import pallas as pl
from jax.experimental.pallas import tpu as pltpu
from jax.sharding import PartitionSpec as P

GRID_AXES = ('row', 'col')
MESH = pl.DeviceIdType.MESH
F32 = jnp.float32
BF16 = jnp.bfloat16

DEV = 8
TOK = 128
TOP = 8
D = 2048
FF = 512
LE = 32
CAP = 32
ALL = DEV * TOK
SLOTS = LE * CAP
CW = 512
NC = D // CW
GE = 8
NG = LE // GE
PIECES = NC * NG
RING = 6
HALF = TOK // 2
BF16_MAX = 3.3895313892515355e38


def kernel(tokens, meta, w_in, w_out, out, tok, meta_all, pos_t, lhs, expand, sel, gsel, buf, hacc, hid, o_buf, part, core_in,
           x_in, y_in, z_in, ring, w_sem, t_sem, m_send, m_recv, a_send, a_recv, r_send, r_recv):
    y = lax.axis_index('row')
    col = lax.axis_index('col')
    x = col // 2
    k = col % 2
    g = y * 4 + col

    def place(dy, dx, dk):
        return (1 - y if dy else y), (1 - x if dx else x), (1 - k if dk else k)

    def dev(dy, dx, dk):
        yy, xx, kk = place(dy, dx, dk)
        return {'row': yy, 'col': xx * 2 + kk}

    def block(dy, dx, dk):
        yy, xx, kk = place(dy, dx, dk)
        return kk * 4 + yy * 2 + xx

    def rows(dy, dx, dk):
        return pl.ds(pl.multiple_of(block(dy, dx, dk) * TOK, TOK), TOK)

    def half_rows(dy, dx, dk, h):
        return pl.ds(pl.multiple_of(block(dy, dx, dk) * TOK + h * HALF, HALF), HALF)

    own = block(0, 0, 0)

    def tok_copy(c):
        return pltpu.make_async_copy(tokens.at[:, pl.ds(c * CW, CW)], tok.at[c, rows(0, 0, 0)], t_sem.at[c])

    for c in range(NC):
        tok_copy(c).start()

    def in_copy(p, slot):
        c, gr = p // NG, p % NG
        return pltpu.make_async_copy(
            w_in.at[pl.ds(gr * GE, GE), pl.ds(pl.multiple_of(c * CW, CW), CW), :], ring.at[slot], w_sem.at[slot])

    def out_copy(p, slot):
        c, gr = p // NG, p % NG
        return pltpu.make_async_copy(
            w_out.at[pl.ds(gr * GE, GE), :, pl.ds(pl.multiple_of(c * CW, CW), CW)], ring.at[slot], w_sem.at[slot])

    for p in range(RING):
        in_copy(p, p).start()

    def refill(p, slot):
        nxt = p + RING

        @pl.when(nxt < PIECES)
        def _():
            in_copy(nxt, slot).start()

        @pl.when(jnp.logical_and(nxt >= PIECES, nxt < 2 * PIECES))
        def _():
            out_copy(nxt - PIECES, slot).start()

    rel = [(dy, dx, dk) for dy in (0, 1) for dx in (0, 1) for dk in (0, 1)]
    barrier = pltpu.get_barrier_semaphore()
    for r in rel[1:]:
        pl.semaphore_signal(barrier, inc=1, device_id=dev(*r), device_id_type=MESH)
    pl.semaphore_wait(barrier, DEV - 1)

    def meta_copy(i, dst):
        return pltpu.make_async_remote_copy(meta, meta_all.at[dst], m_send.at[i], m_recv.at[i], device_id=dev(*rel[i]),
                                            device_id_type=MESH)

    for i in range(1, DEV):
        meta_copy(i, own).start()

    def a_copy(c, i, region, to):
        ref = tok.at[c, region]
        return pltpu.make_async_remote_copy(ref, ref, a_send.at[c, i], a_recv.at[c, i], device_id=dev(*to), device_id_type=MESH)

    A_SENT = [((0, 0, 0), None, (0, 0, 1)), ((0, 0, 0), None, (0, 1, 0)), ((0, 0, 0), None, (1, 0, 0)),
              ((0, 1, 0), None, (0, 0, 1)), ((0, 1, 0), 0, (1, 0, 0)), ((1, 0, 0), None, (0, 0, 1)),
              ((1, 0, 0), 1, (0, 1, 0)), ((1, 1, 0), None, (0, 0, 1))]
    A_GOT = [((0, 0, 1), None), ((0, 1, 0), None), ((1, 0, 0), None), ((0, 1, 1), None), ((1, 1, 0), 0), ((1, 0, 1), None),
             ((1, 1, 0), 1), ((1, 1, 1), None)]

    def region(where, h):
        return rows(*where) if h is None else half_rows(*where, h)

    def a_start(c, i):
        where, h, to = A_SENT[i]
        a_copy(c, i, region(where, h), to).start()

    def a_wait_send(c, i):
        where, h, to = A_SENT[i]
        a_copy(c, i, region(where, h), to).wait_send()

    def a_wait(c, i):
        where, h = A_GOT[i]
        a_copy(c, i, region(where, h), A_SENT[i][2]).wait_recv()

    def a_own(c):
        tok_copy(c).wait()
        for i in (1, 2, 0):
            a_start(c, i)

    def a_forward(c):
        a_wait(c, 1)
        a_start(c, 4)
        a_start(c, 3)
        a_wait(c, 2)
        a_start(c, 6)
        a_start(c, 5)

    def a_corner(c):
        a_wait(c, 4)
        a_wait(c, 6)
        a_start(c, 7)

    a_own(0)
    a_own(1)

    lane = lax.broadcasted_iota(jnp.int32, (TOK, SLOTS), 1)
    sub = lax.broadcasted_iota(jnp.int32, (TOK, SLOTS), 0)
    lane_expert = lax.shift_right_logical(lane, 5)
    for q in range(4):
        expand[q] = jnp.where(sub - LE * q == lane_expert, 1.0, 0.0).astype(BF16)
    hacc[...] = jnp.zeros_like(hacc)
    meta_all[own] = meta[...]

    for i in range(1, DEV):
        meta_copy(i, block(*rel[i])).wait_recv()

    eid = (g * LE + lax.broadcasted_iota(jnp.int32, (LE, 1), 0)).astype(F32)
    upper = jnp.where(lax.broadcasted_iota(jnp.int32, (TOK, TOK), 0) < lax.broadcasted_iota(jnp.int32, (TOK, TOK), 1), 1.0, 0.0)
    upper = upper.astype(BF16)
    before = jnp.zeros((LE, 1), F32)
    for gi in range(DEV):
        b = (gi % 2) * 4 + (gi // 4) * 2 + (gi % 4) // 2
        chose = jnp.zeros((LE, TOK), F32)
        gate = jnp.zeros((LE, TOK), F32)
        for j in range(TOP):
            hit = meta_all[b, j:j + 1, :] == eid
            chose = chose + jnp.where(hit, 1.0, 0.0)
            gate = gate + jnp.where(hit, meta_all[b, TOP + j:TOP + j + 1, :], 0.0)
        rank = jnp.dot(chose.astype(BF16), upper, preferred_element_type=F32) + before
        before = before + jnp.sum(chose, axis=1, keepdims=True)
        pos = jnp.where(jnp.logical_and(chose > 0.0, rank < float(CAP)), rank, -1.0)
        pos_t[:, b * TOK:(b + 1) * TOK] = pos
        high = jnp.minimum(gate, BF16_MAX).astype(BF16).astype(F32)
        rest = gate - high
        mid = rest.astype(BF16).astype(F32)
        low = rest - mid
        table = jnp.concatenate([pos, high, mid, low], axis=0)
        lhs[b * TOK:(b + 1) * TOK, :] = table.T.astype(BF16)

    slot_rank = lax.broadcasted_iota(jnp.int32, (CAP, ALL), 0).astype(F32)

    def sel_step(e, _):
        row = pos_t[pl.ds(e, 1), :]
        sel[pl.ds(pl.multiple_of(e * CAP, CAP), CAP), :] = jnp.where(row == slot_rank, 1.0, 0.0).astype(BF16)
        return 0

    lax.fori_loop(0, LE, sel_step, 0)

    a_forward(0)
    a_own(2)

    lane_rank = jnp.bitwise_and(lax.broadcasted_iota(jnp.int32, (TOK, SLOTS), 1), CAP - 1).astype(F32)

    def gate_step(b, _):
        rr = pl.ds(pl.multiple_of(b * TOK, TOK), TOK)
        table = lhs[rr, :]
        mine = jnp.dot(table, expand[0], preferred_element_type=F32) == lane_rank
        for q in range(3):
            val = jnp.dot(table, expand[q + 1], preferred_element_type=F32)
            gsel[q, rr, :] = jnp.where(mine, val, 0.0).astype(BF16)
        return 0

    lax.fori_loop(0, DEV, gate_step, 0)
    a_corner(0)

    def expert_rows(gr, i):
        return pl.ds(pl.multiple_of((gr * GE + i) * CAP, CAP), CAP)

    def first_chunk(c, _):
        for i in (0, 3, 5, 7):
            a_wait(c, i)

        def dispatch(mb, _):
            rr = pl.ds(pl.multiple_of(mb * 256, 256), 256)
            buf[rr, :] = jnp.dot(sel[rr, :], tok[c], preferred_element_type=F32).astype(BF16)
            return 0

        lax.fori_loop(0, SLOTS // 256, dispatch, 0)

        def group(gr, _):
            @pl.when(jnp.logical_and(gr == 1, c + 1 < NC))
            def _():
                a_forward(c + 1)

            @pl.when(jnp.logical_and(gr == 1, c + 3 < NC))
            def _():
                a_own(c + 3)

            @pl.when(jnp.logical_and(gr == 3, c + 1 < NC))
            def _():
                a_corner(c + 1)

            p = c * NG + gr
            slot = p % RING
            in_copy(p, slot).wait()
            for i in range(GE):
                rr = expert_rows(gr, i)
                hacc[rr, :] += jnp.dot(buf[rr, :], ring[slot, i], preferred_element_type=F32)
            refill(p, slot)
            return 0

        lax.fori_loop(0, NG, group, 0)
        return 0

    lax.fori_loop(0, NC, first_chunk, 0)

    def act(mb, _):
        rr = pl.ds(pl.multiple_of(mb * 128, 128), 128)
        hid[rr, :] = jax.nn.gelu(hacc[rr, :]).astype(BF16)
        return 0

    lax.fori_loop(0, SLOTS // 128, act, 0)

    def core_copy(c):
        src = part.at[c, pl.ds(pl.multiple_of((1 - k) * 4 * TOK, 4 * TOK), 4 * TOK)]
        return pltpu.make_async_remote_copy(src, core_in.at[c], r_send.at[c, 0], r_recv.at[c, 0], device_id=dev(0, 0, 1),
                                            device_id_type=MESH)

    def r_copy(c, i, where, h, dst, to):
        return pltpu.make_async_remote_copy(part.at[c, half_rows(*where, h)], dst, r_send.at[c, i], r_recv.at[c, i],
                                            device_id=dev(*to), device_id_type=MESH)

    def r_copies(c):
        return [r_copy(c, 1, (1, 1, 0), 0, x_in.at[c, 1], (0, 1, 0)),
                r_copy(c, 2, (1, 1, 0), 1, y_in.at[c, 1], (1, 0, 0)),
                r_copy(c, 3, (0, 1, 0), 0, x_in.at[c, 0], (0, 1, 0)),
                r_copy(c, 4, (1, 0, 0), 1, y_in.at[c, 0], (1, 0, 0)),
                r_copy(c, 5, (1, 0, 0), 0, z_in.at[c, 0], (1, 0, 0)),
                r_copy(c, 6, (0, 1, 0), 1, z_in.at[c, 1], (0, 1, 0))]

    def r_first(c):
        core_copy(c).wait_recv()
        base = k * 4 * TOK

        def add(i, _):
            rr = pl.ds(pl.multiple_of(base + i * TOK, TOK), TOK)
            part[c, rr, :] = part[c, rr, :] + core_in[c, pl.ds(pl.multiple_of(i * TOK, TOK), TOK), :]
            return 0

        lax.fori_loop(0, 4, add, 0)
        cs = r_copies(c)
        for i in range(4):
            cs[i].start()

    def r_second(c):
        cs = r_copies(c)
        cs[0].wait_recv()
        rr = half_rows(1, 0, 0, 0)
        part[c, rr, :] = part[c, rr, :] + x_in[c, 1]
        cs[4].start()
        cs[1].wait_recv()
        rr = half_rows(0, 1, 0, 1)
        part[c, rr, :] = part[c, rr, :] + y_in[c, 1]
        cs[5].start()

    def r_last(c):
        cs = r_copies(c)
        for i in range(2, 6):
            cs[i].wait_recv()
        for h, near in ((0, x_in), (1, y_in)):
            rr = half_rows(0, 0, 0, h)
            total = part[c, rr, :] + near[c, 0] + z_in[c, h]
            total = tok[c, rr, :].astype(F32) + total
            out[h * HALF:(h + 1) * HALF, pl.ds(pl.multiple_of(c * CW, CW), CW)] = total.astype(BF16)

    def second_chunk(c, _):
        def group(gr, _):
            @pl.when(jnp.logical_and(gr == 1, c >= 1))
            def _():
                r_first(c - 1)

            @pl.when(jnp.logical_and(gr == 3, c >= 2))
            def _():
                r_second(c - 2)

            p = PIECES + c * NG + gr
            slot = p % RING
            out_copy(p - PIECES, slot).wait()
            for i in range(GE):
                rr = expert_rows(gr, i)
                o_buf[rr, :] = jnp.dot(hid[rr, :], ring[slot, i], preferred_element_type=F32).astype(BF16)
            refill(p, slot)
            return 0

        lax.fori_loop(0, NG, group, 0)

        def combine(mb, _):
            rr = pl.ds(pl.multiple_of(mb * 256, 256), 256)
            o = o_buf[...]
            acc = jnp.dot(gsel[0, rr, :], o, preferred_element_type=F32)
            acc = acc + jnp.dot(gsel[1, rr, :], o, preferred_element_type=F32)
            acc = acc + jnp.dot(gsel[2, rr, :], o, preferred_element_type=F32)
            part[c, rr, :] = acc
            return 0

        lax.fori_loop(0, ALL // 256, combine, 0)
        core_copy(c).start()
        return 0

    lax.fori_loop(0, NC, second_chunk, 0)
    r_first(NC - 1)
    r_second(NC - 2)

    def finish(c, _):
        r_last(c)
        return 0

    lax.fori_loop(0, NC - 1, finish, 0)
    r_second(NC - 1)
    r_last(NC - 1)

    for i in range(1, DEV):
        meta_copy(i, own).wait_send()

    def drain(c, _):
        for i in range(8):
            a_wait_send(c, i)
        core_copy(c).wait_send()
        for cp in r_copies(c):
            cp.wait_send()
        return 0

    lax.fori_loop(0, NC, drain, 0)


def solution(mesh):
    def device_fn(tokens, expert_ids, gate_weights, w_in, w_out):
        meta = jnp.concatenate([expert_ids.astype(F32), gate_weights], axis=1).T
        dma = pltpu.SemaphoreType.DMA
        any_spec = pl.BlockSpec(memory_space=pl.ANY)
        vmem_spec = pl.BlockSpec(memory_space=pltpu.VMEM)
        return pl.pallas_call(
            kernel,
            out_shape=jax.ShapeDtypeStruct((TOK, D), BF16),
            in_specs=[any_spec, vmem_spec, any_spec, any_spec],
            out_specs=vmem_spec,
            scratch_shapes=[
                pltpu.VMEM((NC, ALL, CW), BF16),
                pltpu.VMEM((DEV, 2 * TOP, TOK), F32),
                pltpu.VMEM((LE, ALL), F32),
                pltpu.VMEM((ALL, TOK), BF16),
                pltpu.VMEM((4, TOK, SLOTS), BF16),
                pltpu.VMEM((SLOTS, ALL), BF16),
                pltpu.VMEM((3, ALL, SLOTS), BF16),
                pltpu.VMEM((SLOTS, CW), BF16),
                pltpu.VMEM((SLOTS, FF), F32),
                pltpu.VMEM((SLOTS, FF), BF16),
                pltpu.VMEM((SLOTS, CW), BF16),
                pltpu.VMEM((NC, ALL, CW), F32),
                pltpu.VMEM((NC, ALL // 2, CW), F32),
                pltpu.VMEM((NC, 2, HALF, CW), F32),
                pltpu.VMEM((NC, 2, HALF, CW), F32),
                pltpu.VMEM((NC, 2, HALF, CW), F32),
                pltpu.VMEM((RING, GE, 512, CW), BF16),
                dma((RING,)), dma((NC,)), dma((DEV,)), dma((DEV,)), dma((NC, 8)), dma((NC, 8)), dma((NC, 7)), dma((NC, 7)),
            ],
            compiler_params=pltpu.CompilerParams(collective_id=0, has_side_effects=True, vmem_limit_bytes=67043328),
            name='experts',
        )(tokens, meta, w_in, w_out)

    token_spec = P(('data', 'row', 'col'), None)
    expert_spec = P(GRID_AXES, None, None)
    return jax.shard_map(device_fn, mesh=mesh, in_specs=(token_spec, token_spec, token_spec, expert_spec, expert_spec),
                         out_specs=token_spec, check_vma=False)
```

time: 381 us -> 103 us (0.27)
  waiting for transfers between devices: 182 us -> 0 us
  Pallas kernels: 0 us -> 98.8 us
  local copies, waits for them, and re-layouts: 90.4 us -> 1.88 us
  matrix products: 52.6 us -> 0 us
  other arithmetic: 32 us -> 1.97 us
  blocking collectives: 14 us -> 0 us
  starting transfers between devices: 9.99 us -> 0 us
    all_to_all x3 -> x0, waiting for transfers between devices: 182 us -> none  [the longest x1 93.6 us: device_fn(): returned = lax.all_to_all(back_rows, GRID_AXES, 0, 0, tiled=True)]
    pallas_call x0 -> x1, Pallas kernels: none -> 98.8 us  [device_fn(): pl.pallas_call(kernel, out_shape=jax.ShapeDtypeStruct((TOK, D), BF16), in...]
    gather x9 -> x0, local copies, waits for them, and re-layouts: 79.6 us -> none  [the longest x1 19.1 us: device_fn(): jnp.take(expert_out.reshape(-1, model_width), back_index.reshape(-1), axi...]
    dot_general x3 -> x0, matrix products: 52.6 us -> none  [the longest x1 25.7 us: device_fn(): jnp.einsum('ecf,efd->ecd', hidden, w_out, preferred_element_type=jnp.floa...]
    select_n x8 -> x0, other arithmetic: 17.3 us -> none  [the longest x2 7.29 us: device_fn(): jnp.take(expert_out.reshape(-1, model_width), back_index.reshape(-1), axi...]
    all_gather x2 -> x0, blocking collectives: 14 us -> none  [the longest x1 9.8 us: device_fn(): col_counts = lax.all_gather(counts, 'col')]
    all_to_all x3 -> x0, starting transfers between devices: 9.99 us -> none  [the longest x1 4.05 us: device_fn(): returned = lax.all_to_all(back_rows, GRID_AXES, 0, 0, tiled=True)]
    scatter x2 -> x0, local copies, waits for them, and re-layouts: 8.63 us -> none  [the longest x1 4.32 us: device_fn(): jnp.full((num_experts * per_source,), tok_dev, jnp.int32).at[send_pos]]
  transfers between devices with their start and end apart: 3 -> 0, of which waited for: 2 -> 0; matrix products, arithmetic and copies ran while one was open for 15% -> 0% of each run, Pallas kernels for 0% -> 0%
where the time goes in v1:
time: 103 us
  Pallas kernels  98.8 us (96%)
  other arithmetic  1.97 us (2%)
  local copies, waits for them, and re-layouts  1.88 us (2%)
    pallas_call x1, Pallas kernels, device_fn(): pl.pallas_call(kernel, out_shape=jax.ShapeDtypeStruct((TOK, D), BF16), in...  98.8 us

profile of v1, /device:TPU:0, one launch (start us, length us, event | category | flops | bytes accessed | tf_op | source)
XLA Modules:
  0.0 102.7 jit_solution(5114859870936241098)
XLA Ops:
  0.0 0.7 convert_element_type.3
  0.7 1.3 %maximum_bitcast_fusion.meta = f32[16,128]{1,0:T(8,128)} fusion(f32[128,8]{0,1:T(8,128)} %param.7, f32[128,8]{0,1:T(8,128)S(1)} %convert_element_type.3), kind=kLoop, calls=%fused_computation | loop fusion | flops 2048 | bytes 16384 | tf_op jit(solution)/shard_map/transpose | solution.py:370
  2.0 98.8 %experts.1 = bf16[128,2048]{1,0:T(8,128)(2,1)} custom-call(bf16[128,2048]{1,0:T(8,128)(2,1)} %tokens.1, f32[16,128]{1,0:T(8,128)} %maximum_bitcast_fusion.meta, bf16[32,2048,512]{2,1,0:T(8,128)(2,1)} %w_in.1, bf16[32,512,2048]{2,1,0:T(8,128)(2,1)} %w_out.1), custom_call_target="tpu_custom_call" | custom-call | tf_op jit(solution)/shard_map/experts/pallas_call | solution.py:374
  100.8 1.9 %copy.7 = bf16[128,2048]{1,0:T(8,128)(2,1)} copy(bf16[128,2048]{1,0:T(8,128)(2,1)} %experts.1) | data formatting | bytes 1048576

commit v2 on v1

--- a/solution.py
+++ b/solution.py
@@ -25,11 +25,13 @@
 NG = LE // GE
 PIECES = NC * NG
 RING = 6
+CW2 = 256
+NC2 = D // CW2
 HALF = TOK // 2
 BF16_MAX = 3.3895313892515355e38
 
 
-def kernel(tokens, meta, w_in, w_out, out, tok, meta_all, pos_t, lhs, expand, sel, gsel, buf, hacc, hid, o_buf, part, core_in,
+def kernel(tokens, ids, gates, w_in, w_out, out, tok, meta, meta_all, pos_t, lhs, expand, sel, gsel, buf, hacc, hid, o_buf, part, core_in,
            x_in, y_in, z_in, ring, w_sem, t_sem, m_send, m_recv, a_send, a_recv, r_send, r_recv):
     y = lax.axis_index('row')
     col = lax.axis_index('col')
@@ -85,6 +87,9 @@
         @pl.when(jnp.logical_and(nxt >= PIECES, nxt < 2 * PIECES))
         def _():
             out_copy(nxt - PIECES, slot).start()
+
+    meta[0:TOP, :] = ids[...].astype(F32)
+    meta[TOP:2 * TOP, :] = gates[...]
 
     rel = [(dy, dx, dk) for dy in (0, 1) for dx in (0, 1) for dk in (0, 1)]
     barrier = pltpu.get_barrier_semaphore()
@@ -179,6 +184,9 @@
         table = jnp.concatenate([pos, high, mid, low], axis=0)
         lhs[b * TOK:(b + 1) * TOK, :] = table.T.astype(BF16)
 
+    a_forward(0)
+    a_own(2)
+
     slot_rank = lax.broadcasted_iota(jnp.int32, (CAP, ALL), 0).astype(F32)
 
     def sel_step(e, _):
@@ -187,9 +195,6 @@
         return 0
 
     lax.fori_loop(0, LE, sel_step, 0)
-
-    a_forward(0)
-    a_own(2)
 
     lane_rank = jnp.bitwise_and(lax.broadcasted_iota(jnp.int32, (TOK, SLOTS), 1), CAP - 1).astype(F32)
 
@@ -202,7 +207,10 @@
             gsel[q, rr, :] = jnp.where(mine, val, 0.0).astype(BF16)
         return 0
 
-    lax.fori_loop(0, DEV, gate_step, 0)
+    lax.fori_loop(0, DEV // 2, gate_step, 0)
+    a_forward(1)
+    a_own(3)
+    lax.fori_loop(DEV // 2, DEV, gate_step, 0)
     a_corner(0)
 
     def expert_rows(gr, i):
@@ -220,15 +228,11 @@
         lax.fori_loop(0, SLOTS // 256, dispatch, 0)
 
         def group(gr, _):
-            @pl.when(jnp.logical_and(gr == 1, c + 1 < NC))
-            def _():
-                a_forward(c + 1)
-
-            @pl.when(jnp.logical_and(gr == 1, c + 3 < NC))
-            def _():
-                a_own(c + 3)
-
-            @pl.when(jnp.logical_and(gr == 3, c + 1 < NC))
+            @pl.when(jnp.logical_and(gr == 1, c + 2 < NC))
+            def _():
+                a_forward(c + 2)
+
+            @pl.when(jnp.logical_and(gr == 2, c + 1 < NC))
             def _():
                 a_corner(c + 1)
 
@@ -258,17 +262,14 @@
         return pltpu.make_async_remote_copy(src, core_in.at[c], r_send.at[c, 0], r_recv.at[c, 0], device_id=dev(0, 0, 1),
                                             device_id_type=MESH)
 
-    def r_copy(c, i, where, h, dst, to):
-        return pltpu.make_async_remote_copy(part.at[c, half_rows(*where, h)], dst, r_send.at[c, i], r_recv.at[c, i],
-                                            device_id=dev(*to), device_id_type=MESH)
-
-    def r_copies(c):
-        return [r_copy(c, 1, (1, 1, 0), 0, x_in.at[c, 1], (0, 1, 0)),
-                r_copy(c, 2, (1, 1, 0), 1, y_in.at[c, 1], (1, 0, 0)),
-                r_copy(c, 3, (0, 1, 0), 0, x_in.at[c, 0], (0, 1, 0)),
-                r_copy(c, 4, (1, 0, 0), 1, y_in.at[c, 0], (1, 0, 0)),
-                r_copy(c, 5, (1, 0, 0), 0, z_in.at[c, 0], (1, 0, 0)),
-                r_copy(c, 6, (0, 1, 0), 1, z_in.at[c, 1], (0, 1, 0))]
+    R_SENT = [None, ((1, 1, 0), 0, 0, 1), ((1, 1, 0), 1, 1, 1), ((0, 1, 0), 0, 0, 0), ((1, 0, 0), 1, 1, 0),
+              ((1, 0, 0), 0, 2, 0), ((0, 1, 0), 1, 2, 1)]
+    R_TO = [None, (0, 1, 0), (1, 0, 0), (0, 1, 0), (1, 0, 0), (1, 0, 0), (0, 1, 0)]
+
+    def r_copy(c, i):
+        where, h, box, at = R_SENT[i]
+        return pltpu.make_async_remote_copy(part.at[c, half_rows(*where, h)], (x_in, y_in, z_in)[box].at[c, at],
+                                            r_send.at[c, i], r_recv.at[c, i], device_id=dev(*R_TO[i]), device_id_type=MESH)
 
     def r_first(c):
         core_copy(c).wait_recv()
@@ -280,48 +281,60 @@
             return 0
 
         lax.fori_loop(0, 4, add, 0)
-        cs = r_copies(c)
-        for i in range(4):
-            cs[i].start()
+        for i in range(1, 5):
+            r_copy(c, i).start()
 
     def r_second(c):
-        cs = r_copies(c)
-        cs[0].wait_recv()
+        r_copy(c, 1).wait_recv()
         rr = half_rows(1, 0, 0, 0)
         part[c, rr, :] = part[c, rr, :] + x_in[c, 1]
-        cs[4].start()
-        cs[1].wait_recv()
+        r_copy(c, 5).start()
+        r_copy(c, 2).wait_recv()
         rr = half_rows(0, 1, 0, 1)
         part[c, rr, :] = part[c, rr, :] + y_in[c, 1]
-        cs[5].start()
+        r_copy(c, 6).start()
 
     def r_last(c):
-        cs = r_copies(c)
-        for i in range(2, 6):
-            cs[i].wait_recv()
+        for i in range(3, 7):
+            r_copy(c, i).wait_recv()
+        wide = c // 2
+        cols = pl.ds(pl.multiple_of((c % 2) * CW2, CW2), CW2)
         for h, near in ((0, x_in), (1, y_in)):
             rr = half_rows(0, 0, 0, h)
             total = part[c, rr, :] + near[c, 0] + z_in[c, h]
-            total = tok[c, rr, :].astype(F32) + total
-            out[h * HALF:(h + 1) * HALF, pl.ds(pl.multiple_of(c * CW, CW), CW)] = total.astype(BF16)
+            total = tok[wide, rr, cols].astype(F32) + total
+            out[h * HALF:(h + 1) * HALF, pl.ds(pl.multiple_of(c * CW2, CW2), CW2)] = total.astype(BF16)
 
     def second_chunk(c, _):
+        wide = c // 2
+        half = c % 2
+        cols = pl.ds(pl.multiple_of(half * CW2, CW2), CW2)
+
         def group(gr, _):
-            @pl.when(jnp.logical_and(gr == 1, c >= 1))
+            @pl.when(jnp.logical_and(gr == 2, c >= 1))
             def _():
                 r_first(c - 1)
 
-            @pl.when(jnp.logical_and(gr == 3, c >= 2))
-            def _():
-                r_second(c - 2)
-
-            p = PIECES + c * NG + gr
+            @pl.when(jnp.logical_and(gr == 3, c >= 3))
+            def _():
+                r_second(c - 3)
+
+            q = wide * NG + gr
+            p = PIECES + q
             slot = p % RING
-            out_copy(p - PIECES, slot).wait()
+
+            @pl.when(half == 0)
+            def _():
+                out_copy(q, slot).wait()
+
             for i in range(GE):
                 rr = expert_rows(gr, i)
-                o_buf[rr, :] = jnp.dot(hid[rr, :], ring[slot, i], preferred_element_type=F32).astype(BF16)
-            refill(p, slot)
+                o_buf[rr, :] = jnp.dot(hid[rr, :], ring[slot, i, :, cols], preferred_element_type=F32).astype(BF16)
+
+            @pl.when(half == 1)
+            def _():
+                refill(p, slot)
+
             return 0
 
         lax.fori_loop(0, NG, group, 0)
@@ -335,21 +348,24 @@
             part[c, rr, :] = acc
             return 0
 
-        lax.fori_loop(0, ALL // 256, combine, 0)
+        lax.fori_loop(2 * (1 - k), 2 * (1 - k) + 2, combine, 0)
         core_copy(c).start()
-        return 0
-
-    lax.fori_loop(0, NC, second_chunk, 0)
-    r_first(NC - 1)
-    r_second(NC - 2)
+        lax.fori_loop(2 * k, 2 * k + 2, combine, 0)
+        return 0
+
+    lax.fori_loop(0, NC2, second_chunk, 0)
+    r_first(NC2 - 1)
+    r_second(NC2 - 3)
 
     def finish(c, _):
         r_last(c)
         return 0
 
-    lax.fori_loop(0, NC - 1, finish, 0)
-    r_second(NC - 1)
-    r_last(NC - 1)
+    lax.fori_loop(0, NC2 - 4, finish, 0)
+    r_second(NC2 - 2)
+    r_last(NC2 - 4)
+    r_second(NC2 - 1)
+    lax.fori_loop(NC2 - 3, NC2, finish, 0)
 
     for i in range(1, DEV):
         meta_copy(i, own).wait_send()
@@ -357,27 +373,31 @@
     def drain(c, _):
         for i in range(8):
             a_wait_send(c, i)
+        return 0
+
+    def r_drain(c, _):
         core_copy(c).wait_send()
-        for cp in r_copies(c):
-            cp.wait_send()
+        for i in range(1, 7):
+            r_copy(c, i).wait_send()
         return 0
 
     lax.fori_loop(0, NC, drain, 0)
+    lax.fori_loop(0, NC2, r_drain, 0)
 
 
 def solution(mesh):
     def device_fn(tokens, expert_ids, gate_weights, w_in, w_out):
-        meta = jnp.concatenate([expert_ids.astype(F32), gate_weights], axis=1).T
         dma = pltpu.SemaphoreType.DMA
         any_spec = pl.BlockSpec(memory_space=pl.ANY)
         vmem_spec = pl.BlockSpec(memory_space=pltpu.VMEM)
         return pl.pallas_call(
             kernel,
             out_shape=jax.ShapeDtypeStruct((TOK, D), BF16),
-            in_specs=[any_spec, vmem_spec, any_spec, any_spec],
+            in_specs=[any_spec, vmem_spec, vmem_spec, any_spec, any_spec],
             out_specs=vmem_spec,
             scratch_shapes=[
                 pltpu.VMEM((NC, ALL, CW), BF16),
+                pltpu.VMEM((2 * TOP, TOK), F32),
                 pltpu.VMEM((DEV, 2 * TOP, TOK), F32),
                 pltpu.VMEM((LE, ALL), F32),
                 pltpu.VMEM((ALL, TOK), BF16),
@@ -387,18 +407,18 @@
                 pltpu.VMEM((SLOTS, CW), BF16),
                 pltpu.VMEM((SLOTS, FF), F32),
                 pltpu.VMEM((SLOTS, FF), BF16),
-                pltpu.VMEM((SLOTS, CW), BF16),
-                pltpu.VMEM((NC, ALL, CW), F32),
-                pltpu.VMEM((NC, ALL // 2, CW), F32),
-                pltpu.VMEM((NC, 2, HALF, CW), F32),
-                pltpu.VMEM((NC, 2, HALF, CW), F32),
-                pltpu.VMEM((NC, 2, HALF, CW), F32),
+                pltpu.VMEM((SLOTS, CW2), BF16),
+                pltpu.VMEM((NC2, ALL, CW2), F32),
+                pltpu.VMEM((NC2, ALL // 2, CW2), F32),
+                pltpu.VMEM((NC2, 2, HALF, CW2), F32),
+                pltpu.VMEM((NC2, 2, HALF, CW2), F32),
+                pltpu.VMEM((NC2, 2, HALF, CW2), F32),
                 pltpu.VMEM((RING, GE, 512, CW), BF16),
-                dma((RING,)), dma((NC,)), dma((DEV,)), dma((DEV,)), dma((NC, 8)), dma((NC, 8)), dma((NC, 7)), dma((NC, 7)),
+                dma((RING,)), dma((NC,)), dma((DEV,)), dma((DEV,)), dma((NC, 8)), dma((NC, 8)), dma((NC2, 7)), dma((NC2, 7)),
             ],
             compiler_params=pltpu.CompilerParams(collective_id=0, has_side_effects=True, vmem_limit_bytes=67043328),
             name='experts',
-        )(tokens, meta, w_in, w_out)
+        )(tokens, expert_ids.T, gate_weights.T, w_in, w_out)
 
     token_spec = P(('data', 'row', 'col'), None)
     expert_spec = P(GRID_AXES, None, None)

time: 103 us -> 89.1 us (0.87)
  Pallas kernels: 98.8 us -> 87.1 us
  other arithmetic: 1.97 us -> 0 us
    pallas_call x1, Pallas kernels: 98.8 us -> 87.1 us  [device_fn(): pl.pallas_call(kernel, out_shape=jax.ShapeDtypeStruct((TOK, D), BF16), in...]
    transpose x1 -> x0, other arithmetic: 1.29 us -> none  [device_fn(): meta = jnp.concatenate([expert_ids.astype(F32), gate_weights], axis=1).T]
where the time goes in v2:
time: 89.1 us; the launch traced here: 89 us
  Pallas kernels  87.1 us (98%)
  local copies, waits for them, and re-layouts  1.88 us (2%)
    pallas_call x1, Pallas kernels, device_fn(): pl.pallas_call(kernel, out_shape=jax.ShapeDtypeStruct((TOK, D), BF16), in...  87.1 us
    unnamed x1, local copies, waits for them, and re-layouts  1.88 us

profile of v2, /device:TPU:0, one launch (start us, length us, event | category | flops | bytes accessed | tf_op | source)
XLA Modules:
  0.0 89.0 jit_solution(4125219185666044420)
XLA Ops:
  0.0 87.1 %experts.1 = bf16[128,2048]{1,0:T(8,128)(2,1)} custom-call(bf16[128,2048]{1,0:T(8,128)(2,1)} %tokens.1, s32[8,128]{1,0:T(8,128)} %bitcast.2, f32[8,128]{1,0:T(8,128)} %bitcast.3, bf16[32,2048,512]{2,1,0:T(8,128)(2,1)} %w_in.1, bf16[32,512,2048]{2,1,0:T(8,128)(2,1)} %w_out.1), custom_call_target="tpu_custom_call" | custom-call | tf_op jit(solution)/shard_map/experts/pallas_call | solution.py:393
  87.1 1.9 %copy.7 = bf16[128,2048]{1,0:T(8,128)(2,1)} copy(bf16[128,2048]{1,0:T(8,128)(2,1)} %experts.1) | data formatting | bytes 1048576

commit v3 on v2

v3 whole, which is shorter than its diff:
```python
import jax
import jax.numpy as jnp
from jax import lax
from jax.experimental import pallas as pl
from jax.experimental.pallas import tpu as pltpu
from jax.sharding import PartitionSpec as P

GRID_AXES = ('row', 'col')
MESH = pl.DeviceIdType.MESH
F32 = jnp.float32
BF16 = jnp.bfloat16

DEV = 8
TOK = 128
TOP = 8
D = 2048
FF = 512
LE = 32
CAP = 32
ALL = DEV * TOK
SLOTS = LE * CAP
CW = 512
NC = D // CW
GE = 8
NG = LE // GE
PIECES = NC * NG * 2
RING = 18
CW2 = 256
NC2 = D // CW2
HALF = TOK // 2
BF16_MAX = 3.3895313892515355e38


def kernel(tokens, ids, gates, w_in, w_out, out, tok, meta, meta_all, gsel, hid, core_in, x_in, y_in, z_in, ring, w_sem, t_sem, m_send, m_recv, a_send, a_recv, r_send, r_recv):
    y = lax.axis_index('row')
    col = lax.axis_index('col')
    x = col // 2
    k = col % 2
    g = y * 4 + col

    def place(dy, dx, dk):
        return (1 - y if dy else y), (1 - x if dx else x), (1 - k if dk else k)

    def dev(dy, dx, dk):
        yy, xx, kk = place(dy, dx, dk)
        return {'row': yy, 'col': xx * 2 + kk}

    def block(dy, dx, dk):
        yy, xx, kk = place(dy, dx, dk)
        return kk * 4 + xx * 2 + yy

    def rows(dy, dx, dk):
        return pl.ds(pl.multiple_of(block(dy, dx, dk) * TOK, TOK), TOK)

    def half_rows(dy, dx, dk, h):
        return pl.ds(pl.multiple_of(block(dy, dx, dk) * TOK + h * HALF, HALF), HALF)

    own = block(0, 0, 0)

    def tok_copy(c):
        return pltpu.make_async_copy(tokens.at[:, pl.ds(c * CW, CW)], tok.at[c, rows(0, 0, 0)], t_sem.at[c])

    for c in range(NC):
        tok_copy(c).start()

    def in_copy(p, slot):
        c, gr, half = p // (2 * NG), (p // 2) % NG, p % 2
        return pltpu.make_async_copy(
            w_in.at[pl.ds(gr * GE, GE), pl.ds(pl.multiple_of(c * CW, CW), CW), pl.ds(pl.multiple_of(half * 256, 256), 256)],
            ring.at[slot], w_sem.at[slot])

    def out_copy(p, slot):
        c, gr = p // NG, p % NG
        return pltpu.make_async_copy(
            w_out.at[pl.ds(gr * GE, GE), :, pl.ds(pl.multiple_of(c * CW2, CW2), CW2)], ring.at[slot], w_sem.at[slot])

    for p in range(RING):
        in_copy(p, p).start()

    def refill(p, slot):
        nxt = p + RING

        @pl.when(nxt < PIECES)
        def _():
            in_copy(nxt, slot).start()

        @pl.when(jnp.logical_and(nxt >= PIECES, nxt < 2 * PIECES))
        def _():
            out_copy(nxt - PIECES, slot).start()

    meta[0:TOP, :] = ids[...].astype(F32)
    meta[TOP:2 * TOP, :] = gates[...]

    rel = [(dy, dx, dk) for dy in (0, 1) for dx in (0, 1) for dk in (0, 1)]
    barrier = pltpu.get_barrier_semaphore()
    for r in rel[1:]:
        pl.semaphore_signal(barrier, inc=1, device_id=dev(*r), device_id_type=MESH)
    pl.semaphore_wait(barrier, DEV - 1)

    def meta_copy(i, dst):
        return pltpu.make_async_remote_copy(meta, meta_all.at[dst], m_send.at[i], m_recv.at[i], device_id=dev(*rel[i]),
                                            device_id_type=MESH)

    for i in range(1, DEV):
        meta_copy(i, own).start()

    def a_copy(c, i, region, to):
        ref = tok.at[c, region]
        return pltpu.make_async_remote_copy(ref, ref, a_send.at[c, i], a_recv.at[c, i], device_id=dev(*to), device_id_type=MESH)

    A_SENT = [((0, 0, 0), None, (0, 0, 1)), ((0, 0, 0), None, (0, 1, 0)), ((0, 0, 0), None, (1, 0, 0)),
              ((0, 1, 0), None, (0, 0, 1)), ((0, 1, 0), 0, (1, 0, 0)), ((1, 0, 0), None, (0, 0, 1)),
              ((1, 0, 0), 1, (0, 1, 0)), ((1, 1, 0), None, (0, 0, 1))]
    A_GOT = [((0, 0, 1), None), ((0, 1, 0), None), ((1, 0, 0), None), ((0, 1, 1), None), ((1, 1, 0), 0), ((1, 0, 1), None),
             ((1, 1, 0), 1), ((1, 1, 1), None)]

    def region(where, h):
        return rows(*where) if h is None else half_rows(*where, h)

    def a_start(c, i):
        where, h, to = A_SENT[i]
        a_copy(c, i, region(where, h), to).start()

    def a_wait_send(c, i):
        where, h, to = A_SENT[i]
        a_copy(c, i, region(where, h), to).wait_send()

    def a_wait(c, i):
        where, h = A_GOT[i]
        a_copy(c, i, region(where, h), A_SENT[i][2]).wait_recv()

    def a_own(c):
        tok_copy(c).wait()
        for i in (1, 2, 0):
            a_start(c, i)

    def a_forward(c):
        a_wait(c, 1)
        a_start(c, 4)
        a_start(c, 3)
        a_wait(c, 2)
        a_start(c, 6)
        a_start(c, 5)

    def a_corner(c):
        a_wait(c, 4)
        a_wait(c, 6)
        a_start(c, 7)

    a_own(0)
    a_own(1)

    def expert_rows(gr, i):
        return pl.ds(pl.multiple_of((gr * GE + i) * CAP, CAP), CAP)

    def gather_and_first(pos_t, lhs, expand, sel, buf, hacc):
        lane = lax.broadcasted_iota(jnp.int32, (TOK, SLOTS), 1)
        sub = lax.broadcasted_iota(jnp.int32, (TOK, SLOTS), 0)
        lane_expert = lax.shift_right_logical(lane, 5)
        for q in range(4):
            expand[q] = jnp.where(sub - LE * q == lane_expert, 1.0, 0.0).astype(BF16)
        hacc[...] = jnp.zeros_like(hacc)
        meta_all[own] = meta[...]

        for i in range(1, DEV):
            meta_copy(i, block(*rel[i])).wait_recv()

        eid = (g * LE + lax.broadcasted_iota(jnp.int32, (LE, 1), 0)).astype(F32)
        upper = jnp.where(lax.broadcasted_iota(jnp.int32, (TOK, TOK), 0) < lax.broadcasted_iota(jnp.int32, (TOK, TOK), 1), 1.0, 0.0)
        upper = upper.astype(BF16)
        before = jnp.zeros((LE, 1), F32)
        for gi in range(DEV):
            b = (gi % 2) * 4 + ((gi % 4) // 2) * 2 + gi // 4
            chose = jnp.zeros((LE, TOK), F32)
            gate = jnp.zeros((LE, TOK), F32)
            for j in range(TOP):
                hit = meta_all[b, j:j + 1, :] == eid
                chose = chose + jnp.where(hit, 1.0, 0.0)
                gate = gate + jnp.where(hit, meta_all[b, TOP + j:TOP + j + 1, :], 0.0)
            rank = jnp.dot(chose.astype(BF16), upper, preferred_element_type=F32) + before
            before = before + jnp.sum(chose, axis=1, keepdims=True)
            pos = jnp.where(jnp.logical_and(chose > 0.0, rank < float(CAP)), rank, -1.0)
            pos_t[:, b * TOK:(b + 1) * TOK] = pos
            high = jnp.minimum(gate, BF16_MAX).astype(BF16).astype(F32)
            rest = gate - high
            mid = rest.astype(BF16).astype(F32)
            low = rest - mid
            table = jnp.concatenate([pos, high, mid, low], axis=0)
            lhs[b * TOK:(b + 1) * TOK, :] = table.T.astype(BF16)

        a_forward(0)
        a_own(2)

        slot_rank = lax.broadcasted_iota(jnp.int32, (CAP, ALL), 0).astype(F32)

        def sel_step(e, _):
            row = pos_t[pl.ds(e, 1), :]
            sel[pl.ds(pl.multiple_of(e * CAP, CAP), CAP), :] = jnp.where(row == slot_rank, 1.0, 0.0).astype(BF16)
            return 0

        lax.fori_loop(0, LE, sel_step, 0)

        lane_rank = jnp.bitwise_and(lax.broadcasted_iota(jnp.int32, (TOK, SLOTS), 1), CAP - 1).astype(F32)

        def gate_step(b, _):
            rr = pl.ds(pl.multiple_of(b * TOK, TOK), TOK)
            table = lhs[rr, :]
            mine = jnp.dot(table, expand[0], preferred_element_type=F32) == lane_rank
            for q in range(3):
                val = jnp.dot(table, expand[q + 1], preferred_element_type=F32)
                gsel[q, rr, :] = jnp.where(mine, val, 0.0).astype(BF16)
            return 0

        lax.fori_loop(0, DEV // 2, gate_step, 0)
        a_forward(1)
        a_own(3)
        lax.fori_loop(DEV // 2, DEV, gate_step, 0)
        a_corner(0)

        def first_chunk(c, _):
            for i in (0, 3, 5, 7):
                a_wait(c, i)

            def dispatch(mb, _):
                rr = pl.ds(pl.multiple_of(mb * 256, 256), 256)
                buf[rr, :] = jnp.dot(sel[rr, :], tok[c], preferred_element_type=F32).astype(BF16)
                return 0

            lax.fori_loop(0, SLOTS // 256, dispatch, 0)

            def group(gr, _):
                @pl.when(jnp.logical_and(gr == 1, c + 2 < NC))
                def _():
                    a_forward(c + 2)

                @pl.when(jnp.logical_and(gr == 2, c + 1 < NC))
                def _():
                    a_corner(c + 1)

                p = (c * NG + gr) * 2
                slot = p % RING
                in_copy(p, slot).wait()
                in_copy(p + 1, slot + 1).wait()
                for i in range(GE):
                    rr = expert_rows(gr, i)
                    for h in range(2):
                        hacc[rr, h * 256:(h + 1) * 256] += jnp.dot(buf[rr, :], ring[slot + h, i], preferred_element_type=F32)
                refill(p, slot)
                refill(p + 1, slot + 1)
                return 0

            lax.fori_loop(0, NG, group, 0)
            return 0

        lax.fori_loop(0, NC, first_chunk, 0)

        def act(mb, _):
            rr = pl.ds(pl.multiple_of(mb * 128, 128), 128)
            hid[rr, :] = jax.nn.gelu(hacc[rr, :]).astype(BF16)
            return 0

        lax.fori_loop(0, SLOTS // 128, act, 0)

    pl.run_scoped(gather_and_first, pltpu.VMEM((LE, ALL), F32), pltpu.VMEM((ALL, TOK), BF16), pltpu.VMEM((4, TOK, SLOTS), BF16),
                  pltpu.VMEM((SLOTS, ALL), BF16), pltpu.VMEM((SLOTS, CW), BF16), pltpu.VMEM((SLOTS, FF), F32))

    def second_and_scatter(o_buf, part):
        def r_copy(c, i):
            src, dst, to = (
                (part.at[c, 1 - k], core_in.at[c], (0, 0, 1)),
                (part.at[c, k, 1 - x, :, 0], x_in.at[c], (0, 1, 0)),
                (part.at[c, k, :, 1 - y, 1], y_in.at[c], (1, 0, 0)),
                (part.at[c, k, x, 1 - y, 0], z_in.at[c, 0], (1, 0, 0)),
                (part.at[c, k, 1 - x, y, 1], z_in.at[c, 1], (0, 1, 0)),
            )[i]
            return pltpu.make_async_remote_copy(src, dst, r_send.at[c, i], r_recv.at[c, i], device_id=dev(*to), device_id_type=MESH)

        def r_first(c):
            r_copy(c, 0).wait_recv()

            def add(i, _):
                part[c, k, i] = part[c, k, i] + core_in[c, i]
                return 0

            lax.fori_loop(0, 2, add, 0)
            r_copy(c, 1).start()
            r_copy(c, 2).start()

        def r_second(c):
            r_copy(c, 1).wait_recv()
            part[c, k, x, 1 - y, 0] = part[c, k, x, 1 - y, 0] + x_in[c, 1 - y]
            r_copy(c, 3).start()
            r_copy(c, 2).wait_recv()
            part[c, k, 1 - x, y, 1] = part[c, k, 1 - x, y, 1] + y_in[c, 1 - x]
            r_copy(c, 4).start()

        def r_last(c):
            r_copy(c, 3).wait_recv()
            r_copy(c, 4).wait_recv()
            wide = c // 2
            cols = pl.ds(pl.multiple_of((c % 2) * CW2, CW2), CW2)
            for h in (0, 1):
                near = x_in[c, y] if h == 0 else y_in[c, x]
                total = part[c, k, x, y, h] + near + z_in[c, h]
                total = tok[wide, half_rows(0, 0, 0, h), cols].astype(F32) + total
                out[h * HALF:(h + 1) * HALF, pl.ds(pl.multiple_of(c * CW2, CW2), CW2)] = total.astype(BF16)

        def second_chunk(c, _):
            def group(gr, _):
                @pl.when(jnp.logical_and(gr == 1, c >= 3))
                def _():
                    r_second(c - 3)

                @pl.when(jnp.logical_and(gr == 3, c >= 1))
                def _():
                    r_first(c - 1)

                q = c * NG + gr
                p = PIECES + q
                slot = p % RING
                out_copy(q, slot).wait()
                for i in range(GE):
                    rr = expert_rows(gr, i)
                    o_buf[rr, :] = jnp.dot(hid[rr, :], ring[slot, i], preferred_element_type=F32).astype(BF16)
                refill(p, slot)
                return 0

            lax.fori_loop(0, NG, group, 0)

            def combine(mb, core):
                rr = pl.ds(pl.multiple_of(core * 512 + mb * 256, 256), 256)
                o = o_buf[...]
                acc = jnp.dot(gsel[0, rr, :], o, preferred_element_type=F32)
                acc = acc + jnp.dot(gsel[1, rr, :], o, preferred_element_type=F32)
                acc = acc + jnp.dot(gsel[2, rr, :], o, preferred_element_type=F32)
                part[c, core, mb] = acc.reshape(2, 2, HALF, CW2)
                return core

            lax.fori_loop(0, 2, combine, 1 - k)
            r_copy(c, 0).start()
            lax.fori_loop(0, 2, combine, k)
            return 0

        lax.fori_loop(0, NC2, second_chunk, 0)
        r_first(NC2 - 1)
        r_second(NC2 - 3)

        def finish(c, _):
            r_last(c)
            return 0

        lax.fori_loop(0, NC2 - 4, finish, 0)
        r_second(NC2 - 2)
        r_last(NC2 - 4)
        r_second(NC2 - 1)
        lax.fori_loop(NC2 - 3, NC2, finish, 0)

        def r_drain(c, _):
            for i in range(5):
                r_copy(c, i).wait_send()
            return 0

        lax.fori_loop(0, NC2, r_drain, 0)

    pl.run_scoped(second_and_scatter, pltpu.VMEM((SLOTS, CW2), BF16), pltpu.VMEM((NC2, 2, 2, 2, 2, HALF, CW2), F32))

    for i in range(1, DEV):
        meta_copy(i, own).wait_send()

    def drain(c, _):
        for i in range(8):
            a_wait_send(c, i)
        return 0

    lax.fori_loop(0, NC, drain, 0)


def solution(mesh):
    def device_fn(tokens, expert_ids, gate_weights, w_in, w_out):
        dma = pltpu.SemaphoreType.DMA
        any_spec = pl.BlockSpec(memory_space=pl.ANY)
        vmem_spec = pl.BlockSpec(memory_space=pltpu.VMEM)
        return pl.pallas_call(
            kernel,
            out_shape=jax.ShapeDtypeStruct((TOK, D), BF16),
            in_specs=[any_spec, vmem_spec, vmem_spec, any_spec, any_spec],
            out_specs=vmem_spec,
            scratch_shapes=[
                pltpu.VMEM((NC, ALL, CW), BF16),
                pltpu.VMEM((2 * TOP, TOK), F32),
                pltpu.VMEM((DEV, 2 * TOP, TOK), F32),
                pltpu.VMEM((3, ALL, SLOTS), BF16),
                pltpu.VMEM((SLOTS, FF), BF16),
                pltpu.VMEM((NC2, 2, 2, 2, HALF, CW2), F32),
                pltpu.VMEM((NC2, 2, HALF, CW2), F32),
                pltpu.VMEM((NC2, 2, HALF, CW2), F32),
                pltpu.VMEM((NC2, 2, HALF, CW2), F32),
                pltpu.VMEM((RING, GE, 512, 256), BF16),
                dma((RING,)), dma((NC,)), dma((DEV,)), dma((DEV,)), dma((NC, 8)), dma((NC, 8)), dma((NC2, 5)), dma((NC2, 5)),
            ],
            compiler_params=pltpu.CompilerParams(collective_id=0, has_side_effects=True, vmem_limit_bytes=67043328),
            name='experts',
        )(tokens, expert_ids.T, gate_weights.T, w_in, w_out)

    token_spec = P(('data', 'row', 'col'), None)
    expert_spec = P(GRID_AXES, None, None)
    return jax.shard_map(device_fn, mesh=mesh, in_specs=(token_spec, token_spec, token_spec, expert_spec, expert_spec),
                         out_specs=token_spec, check_vma=False)
```

time: 89.1 us -> 87.1 us (0.978)
  Pallas kernels: 87.1 us -> 85 us
    pallas_call x1, Pallas kernels: 87.1 us -> 85 us  [device_fn(): pl.pallas_call(kernel, out_shape=jax.ShapeDtypeStruct((TOK, D), BF16), in...]
where the time goes in v3:
time: 87.1 us; the launch traced here: 86.9 us
  Pallas kernels  85 us (98%)
  local copies, waits for them, and re-layouts  1.88 us (2%)
    pallas_call x1, Pallas kernels, device_fn(): pl.pallas_call(kernel, out_shape=jax.ShapeDtypeStruct((TOK, D), BF16), in...  85 us
    unnamed x1, local copies, waits for them, and re-layouts  1.88 us

profile of v3, /device:TPU:0, one launch (start us, length us, event | category | flops | bytes accessed | tf_op | source)
XLA Modules:
  0.0 86.9 jit_solution(10167023687901214738)
XLA Ops:
  0.0 85.0 %experts.1 = bf16[128,2048]{1,0:T(8,128)(2,1)} custom-call(bf16[128,2048]{1,0:T(8,128)(2,1)} %tokens.1, s32[8,128]{1,0:T(8,128)} %bitcast.2, f32[8,128]{1,0:T(8,128)} %bitcast.3, bf16[32,2048,512]{2,1,0:T(8,128)(2,1)} %w_in.1, bf16[32,512,2048]{2,1,0:T(8,128)(2,1)} %w_out.1), custom_call_target="tpu_custom_call" | custom-call | tf_op jit(solution)/shard_map/experts/pallas_call | solution.py:383
  85.0 1.9 %copy.7 = bf16[128,2048]{1,0:T(8,128)(2,1)} copy(bf16[128,2048]{1,0:T(8,128)(2,1)} %experts.1) | data formatting | bytes 1048576

commit v4 on v3

--- a/solution.py
+++ b/solution.py
@@ -221,35 +221,33 @@
             for i in (0, 3, 5, 7):
                 a_wait(c, i)
 
-            def dispatch(mb, _):
-                rr = pl.ds(pl.multiple_of(mb * 256, 256), 256)
-                buf[rr, :] = jnp.dot(sel[rr, :], tok[c], preferred_element_type=F32).astype(BF16)
-                return 0
-
-            lax.fori_loop(0, SLOTS // 256, dispatch, 0)
-
-            def group(gr, _):
-                @pl.when(jnp.logical_and(gr == 1, c + 2 < NC))
+            for mb in range(2):
+                buf[mb * 512:(mb + 1) * 512, :] = jnp.dot(sel[mb * 512:(mb + 1) * 512, :], tok[c],
+                                                          preferred_element_type=F32).astype(BF16)
+
+            def groups(gg, _):
+                @pl.when(jnp.logical_and(gg == 0, c + 2 < NC))
                 def _():
                     a_forward(c + 2)
 
-                @pl.when(jnp.logical_and(gr == 2, c + 1 < NC))
+                @pl.when(jnp.logical_and(gg == 1, c + 1 < NC))
                 def _():
                     a_corner(c + 1)
 
-                p = (c * NG + gr) * 2
-                slot = p % RING
-                in_copy(p, slot).wait()
-                in_copy(p + 1, slot + 1).wait()
-                for i in range(GE):
-                    rr = expert_rows(gr, i)
-                    for h in range(2):
-                        hacc[rr, h * 256:(h + 1) * 256] += jnp.dot(buf[rr, :], ring[slot + h, i], preferred_element_type=F32)
-                refill(p, slot)
-                refill(p + 1, slot + 1)
+                p = (c * NG + gg * 2) * 2
+                for q in range(4):
+                    in_copy(p + q, (p + q) % RING).wait()
+                for u in range(2):
+                    slot = (p + 2 * u) % RING
+                    for i in range(GE):
+                        rr = expert_rows(gg * 2 + u, i)
+                        for h in range(2):
+                            hacc[rr, h * 256:(h + 1) * 256] += jnp.dot(buf[rr, :], ring[slot + h, i], preferred_element_type=F32)
+                for q in range(4):
+                    refill(p + q, (p + q) % RING)
                 return 0
 
-            lax.fori_loop(0, NG, group, 0)
+            lax.fori_loop(0, NG // 2, groups, 0)
             return 0
 
         lax.fori_loop(0, NC, first_chunk, 0)
@@ -306,39 +304,37 @@
                 out[h * HALF:(h + 1) * HALF, pl.ds(pl.multiple_of(c * CW2, CW2), CW2)] = total.astype(BF16)
 
         def second_chunk(c, _):
-            def group(gr, _):
-                @pl.when(jnp.logical_and(gr == 1, c >= 3))
-                def _():
-                    r_second(c - 3)
-
-                @pl.when(jnp.logical_and(gr == 3, c >= 1))
-                def _():
-                    r_first(c - 1)
-
-                q = c * NG + gr
-                p = PIECES + q
-                slot = p % RING
-                out_copy(q, slot).wait()
+            @pl.when(c >= 3)
+            def _():
+                r_second(c - 3)
+
+            p = PIECES + c * NG
+            for q in range(NG):
+                out_copy(c * NG + q, (p + q) % RING).wait()
+            for q in range(NG):
+                slot = (p + q) % RING
                 for i in range(GE):
-                    rr = expert_rows(gr, i)
-                    o_buf[rr, :] = jnp.dot(hid[rr, :], ring[slot, i], preferred_element_type=F32).astype(BF16)
-                refill(p, slot)
-                return 0
-
-            lax.fori_loop(0, NG, group, 0)
-
-            def combine(mb, core):
-                rr = pl.ds(pl.multiple_of(core * 512 + mb * 256, 256), 256)
+                    e = q * GE + i
+                    o_buf[e * CAP:(e + 1) * CAP, :] = jnp.dot(hid[e * CAP:(e + 1) * CAP, :], ring[slot, i],
+                                                              preferred_element_type=F32).astype(BF16)
+            for q in range(NG):
+                refill(p + q, (p + q) % RING)
+
+            @pl.when(c >= 1)
+            def _():
+                r_first(c - 1)
+
+            def combine(core):
+                rr = pl.ds(pl.multiple_of(core * 512, 512), 512)
                 o = o_buf[...]
                 acc = jnp.dot(gsel[0, rr, :], o, preferred_element_type=F32)
                 acc = acc + jnp.dot(gsel[1, rr, :], o, preferred_element_type=F32)
                 acc = acc + jnp.dot(gsel[2, rr, :], o, preferred_element_type=F32)
-                part[c, core, mb] = acc.reshape(2, 2, HALF, CW2)
-                return core
-
-            lax.fori_loop(0, 2, combine, 1 - k)
+                part[c, core] = acc.reshape(2, 2, 2, HALF, CW2)
+
+            combine(1 - k)
             r_copy(c, 0).start()
-            lax.fori_loop(0, 2, combine, k)
+            combine(k)
             return 0
 
         lax.fori_loop(0, NC2, second_chunk, 0)

time: 87.1 us -> 91.9 us (1.055)
  Pallas kernels: 85 us -> 89.8 us
    pallas_call x1, Pallas kernels: 85 us -> 89.8 us  [device_fn(): pl.pallas_call(kernel, out_shape=jax.ShapeDtypeStruct((TOK, D), BF16), in...]
where the time goes in v4:
time: 91.9 us; the launch traced here: 91.7 us
  Pallas kernels  89.8 us (98%)
  local copies, waits for them, and re-layouts  1.88 us (2%)
    pallas_call x1, Pallas kernels, device_fn(): pl.pallas_call(kernel, out_shape=jax.ShapeDtypeStruct((TOK, D), BF16), in...  89.8 us
    unnamed x1, local copies, waits for them, and re-layouts  1.88 us

profile of v4, /device:TPU:0, one launch (start us, length us, event | category | flops | bytes accessed | tf_op | source)
XLA Modules:
  0.0 91.7 jit_solution(9121832585838711466)
XLA Ops:
  0.0 89.8 %experts.1 = bf16[128,2048]{1,0:T(8,128)(2,1)} custom-call(bf16[128,2048]{1,0:T(8,128)(2,1)} %tokens.1, s32[8,128]{1,0:T(8,128)} %bitcast.2, f32[8,128]{1,0:T(8,128)} %bitcast.3, bf16[32,2048,512]{2,1,0:T(8,128)(2,1)} %w_in.1, bf16[32,512,2048]{2,1,0:T(8,128)(2,1)} %w_out.1), custom_call_target="tpu_custom_call" | custom-call | tf_op jit(solution)/shard_map/experts/pallas_call | solution.py:379
  89.8 1.9 %copy.7 = bf16[128,2048]{1,0:T(8,128)(2,1)} copy(bf16[128,2048]{1,0:T(8,128)(2,1)} %experts.1) | data formatting | bytes 1048576

commit v5 on v3

--- a/solution.py
+++ b/solution.py
@@ -24,7 +24,7 @@
 GE = 8
 NG = LE // GE
 PIECES = NC * NG * 2
-RING = 18
+RING = 16
 CW2 = 256
 NC2 = D // CW2
 HALF = TOK // 2
@@ -264,7 +264,7 @@
     pl.run_scoped(gather_and_first, pltpu.VMEM((LE, ALL), F32), pltpu.VMEM((ALL, TOK), BF16), pltpu.VMEM((4, TOK, SLOTS), BF16),
                   pltpu.VMEM((SLOTS, ALL), BF16), pltpu.VMEM((SLOTS, CW), BF16), pltpu.VMEM((SLOTS, FF), F32))
 
-    def second_and_scatter(o_buf, part):
+    def second_and_scatter(o_even, o_odd, part):
         def r_copy(c, i):
             src, dst, to = (
                 (part.at[c, 1 - k], core_in.at[c], (0, 0, 1)),
@@ -305,43 +305,78 @@
                 total = tok[wide, half_rows(0, 0, 0, h), cols].astype(F32) + total
                 out[h * HALF:(h + 1) * HALF, pl.ds(pl.multiple_of(c * CW2, CW2), CW2)] = total.astype(BF16)
 
-        def second_chunk(c, _):
+        def experts_out(c, gr, o_ref):
+            q = c * NG + gr
+            p = PIECES + q
+            slot = p % RING
+            for i in range(GE):
+                rr = expert_rows(gr, i)
+                o_ref[rr, :] = jnp.dot(hid[rr, :], ring[slot, i], preferred_element_type=F32).astype(BF16)
+
+        def combine(c, gr, o_ref):
+            core = (1 - k) + (gr // 2) * (2 * k - 1)
+            mb = gr % 2
+            rr = pl.ds(pl.multiple_of(core * 512 + mb * 256, 256), 256)
+            o = o_ref[...]
+            acc = jnp.dot(gsel[0, rr, :], o, preferred_element_type=F32)
+            acc = acc + jnp.dot(gsel[1, rr, :], o, preferred_element_type=F32)
+            acc = acc + jnp.dot(gsel[2, rr, :], o, preferred_element_type=F32)
+            part[c, core, mb] = acc.reshape(2, 2, HALF, CW2)
+
+        def ready(c, gr):
+            q = c * NG + gr
+            out_copy(q, (PIECES + q) % RING).wait()
+
+        def free(c, gr):
+            p = PIECES + c * NG + gr
+            refill(p, p % RING)
+
+        def handlers(c, gr):
+            @pl.when(jnp.logical_and(gr == 1, c >= 1))
+            def _():
+                r_first(c - 1)
+
+            @pl.when(gr == 2)
+            def _():
+                r_copy(c, 0).start()
+
+            @pl.when(jnp.logical_and(gr == 3, c >= 3))
+            def _():
+                r_second(c - 3)
+
+        def opening(gr, _):
+            ready(0, gr)
+            experts_out(0, gr, o_even)
+            free(0, gr)
+            return 0
+
+        lax.fori_loop(0, NG, opening, 0)
+
+        def both(c, o_here, o_next):
             def group(gr, _):
-                @pl.when(jnp.logical_and(gr == 1, c >= 3))
-                def _():
-                    r_second(c - 3)
-
-                @pl.when(jnp.logical_and(gr == 3, c >= 1))
-                def _():
-                    r_first(c - 1)
-
-                q = c * NG + gr
-                p = PIECES + q
-                slot = p % RING
-                out_copy(q, slot).wait()
-                for i in range(GE):
-                    rr = expert_rows(gr, i)
-                    o_buf[rr, :] = jnp.dot(hid[rr, :], ring[slot, i], preferred_element_type=F32).astype(BF16)
-                refill(p, slot)
+                handlers(c, gr)
+                ready(c + 1, gr)
+                combine(c, gr, o_here)
+                experts_out(c + 1, gr, o_next)
+                free(c + 1, gr)
                 return 0
 
             lax.fori_loop(0, NG, group, 0)
 
-            def combine(mb, core):
-                rr = pl.ds(pl.multiple_of(core * 512 + mb * 256, 256), 256)
-                o = o_buf[...]
-                acc = jnp.dot(gsel[0, rr, :], o, preferred_element_type=F32)
-                acc = acc + jnp.dot(gsel[1, rr, :], o, preferred_element_type=F32)
-                acc = acc + jnp.dot(gsel[2, rr, :], o, preferred_element_type=F32)
-                part[c, core, mb] = acc.reshape(2, 2, HALF, CW2)
-                return core
-
-            lax.fori_loop(0, 2, combine, 1 - k)
-            r_copy(c, 0).start()
-            lax.fori_loop(0, 2, combine, k)
-            return 0
-
-        lax.fori_loop(0, NC2, second_chunk, 0)
+        def pair(i, _):
+            both(2 * i, o_even, o_odd)
+            both(2 * i + 1, o_odd, o_even)
+            return 0
+
+        lax.fori_loop(0, NC2 // 2 - 1, pair, 0)
+        both(NC2 - 2, o_even, o_odd)
+
+        def closing(gr, _):
+            handlers(NC2 - 1, gr)
+            combine(NC2 - 1, gr, o_odd)
+            return 0
+
+        lax.fori_loop(0, NG, closing, 0)
         r_first(NC2 - 1)
         r_second(NC2 - 3)
 
@@ -362,7 +397,8 @@
 
         lax.fori_loop(0, NC2, r_drain, 0)
 
-    pl.run_scoped(second_and_scatter, pltpu.VMEM((SLOTS, CW2), BF16), pltpu.VMEM((NC2, 2, 2, 2, 2, HALF, CW2), F32))
+    pl.run_scoped(second_and_scatter, pltpu.VMEM((SLOTS, CW2), BF16), pltpu.VMEM((SLOTS, CW2), BF16),
+                  pltpu.VMEM((NC2, 2, 2, 2, 2, HALF, CW2), F32))
 
     for i in range(1, DEV):
         meta_copy(i, own).wait_send()

time: 87.1 us -> 87 us (level)
  no operation moved by 1% of the time
where the time goes in v5:
time: 87 us; the launch traced here: 86.9 us
  Pallas kernels  85 us (98%)
  local copies, waits for them, and re-layouts  1.88 us (2%)
    pallas_call x1, Pallas kernels, device_fn(): pl.pallas_call(kernel, out_shape=jax.ShapeDtypeStruct((TOK, D), BF16), in...  85 us
    unnamed x1, local copies, waits for them, and re-layouts  1.88 us

profile of v5, /device:TPU:0, one launch (start us, length us, event | category | flops | bytes accessed | tf_op | source)
XLA Modules:
  0.0 86.9 jit_solution(175727340708325191)
XLA Ops:
  0.0 85.0 %experts.1 = bf16[128,2048]{1,0:T(8,128)(2,1)} custom-call(bf16[128,2048]{1,0:T(8,128)(2,1)} %tokens.1, s32[8,128]{1,0:T(8,128)} %bitcast.2, f32[8,128]{1,0:T(8,128)} %bitcast.3, bf16[32,2048,512]{2,1,0:T(8,128)(2,1)} %w_in.1, bf16[32,512,2048]{2,1,0:T(8,128)(2,1)} %w_out.1), custom_call_target="tpu_custom_call" | custom-call | tf_op jit(solution)/shard_map/experts/pallas_call | solution.py:419
  85.0 1.9 %copy.7 = bf16[128,2048]{1,0:T(8,128)(2,1)} copy(bf16[128,2048]{1,0:T(8,128)(2,1)} %experts.1) | data formatting | bytes 1048576
